TPU v7x, 32 devices: a whole 2x2x4 slice. The times are simulated.
32 devices in a mesh: grp: 4 (over z), pair: 8 (over y, x, core).
Axes of the slice: x: 2, y: 2, z: 4, core: 2. Of those that a mesh axis runs over, the one named last changes fastest.
Arguments:
- amplitudes: bfloat16 [64, 512, 512], P('pair', 'grp'), may hold values from -6 to 6
- cholesky: bfloat16 [512, 512, 2048], P('pair', 'grp'), may hold values from -0.09375 to 0.09375
Outputs:
- ladder_term: float32 [512, 4, 64], P('pair', None, 'grp')
All inputs are finite; a program needn't handle non-finite values.
Results may differ from a plain program's by a relative error of at most 0.003.
Values may be sent and summed in bfloat16 or wider, within the bound.
A program may use at most 128 MiB of HBM per device.

v0:
```python
import jax
import jax.numpy as jnp
from jax import lax
from jax.sharding import PartitionSpec as P

A_WIN = 4


def spread(value, axis, source):
    kept = jnp.where(lax.axis_index(axis) == source, value, 0).astype(value.dtype)
    return lax.psum(kept, axis)


def build_tile(chol_local, portion):
    return lax.dot_general(
        chol_local, portion, (((2,), (2,)), ((), ())), preferred_element_type=jnp.float32
    ).astype(jnp.bfloat16)


def ladder(integrals, amp_part):
    return lax.dot_general(
        integrals, amp_part, (((1, 3), (1, 2)), ((), ())), preferred_element_type=jnp.float32
    )


def per_device(amplitudes, cholesky):
    own_window = cholesky[:A_WIN]
    everyone = lax.all_gather(amplitudes, "pair", axis=0, tiled=True)
    shared = spread(own_window, "pair", 0)
    summed = ladder(
        build_tile(cholesky, lax.all_gather(shared, "grp", axis=1, tiled=True)), everyone
    )
    return lax.psum_scatter(summed, "grp", scatter_dimension=2, tiled=True)


def solution(mesh):
    in_specs = (P("pair", "grp", None), P("pair", "grp", None))
    out_specs = P("pair", None, "grp")
    return jax.shard_map(
        per_device, mesh=mesh, in_specs=in_specs, out_specs=out_specs, check_vma=False
    )
```

profile of v0, /device:TPU:0, one launch (start us, length us, event | category | flops | bytes accessed | tf_op | source)
XLA Modules:
  0.0 360.8 jit_solution(16896979740591227450)
XLA Ops:
  6.5 0.0 copy-start
  6.5 0.0 all-reduce.2.cloned.1.call-start
  6.5 3.1 slice_select_fusion
  9.7 0.0 all-reduce.2.cloned.1.call-update
  9.7 0.0 all-gather.3.cloned.1.call-start
  9.7 65.3 %all-reduce.2.cloned.1.call-done = bf16[4,128,2048]{2,1,0:T(8,128)(2,1)} async-done(((bf16[4,128,2048]{2,1,0:T(8,128)(2,1)}), bf16[4,128,2048]{2,1,0:T(8,128)(2,1)}) %all-reduce.2.cloned.1.call-update) | async-done | bytes 2097168 | tf_op jit(solution)/shard_map/psum | solution.py:11
  75.1 0.0 all-gather.3.cloned.1.call-update
  75.1 0.0 all-gather.5.cloned.1.call-start
  75.2 0.0 copy-done
  75.2 1.6 copy.3
  76.7 0.0 all-gather.5.cloned.1.call-update
  76.7 0.0 reduce-scatter.2.cloned.1.call-start
  76.8 148.6 %all-gather.3.cloned.1.call-done = bf16[4,512,2048]{2,1,0:T(8,128)(2,1)} async-done(((bf16[4,128,2048]{2,1,0:T(8,128)(2,1)}), bf16[4,512,2048]{2,1,0:T(8,128)(2,1)}) %all-gather.3.cloned.1.call-update) | async-done | bytes 8388624 | tf_op jit(solution)/shard_map/all_gather | solution.py:31
  225.4 86.3 %fusion.33 = bf16[64,128,4,512]{3,0,1,2:T(8,128)(2,1)} fusion(bf16[64,128,2048,1]{2,1,0,3:T(8,128)(2,1)} %bitcast.34, bf16[4,512,2048]{2,1,0:T(8,128)(2,1)} %all-gather.3.cloned.1.call-done), kind=kOutput, calls=%fused_computation.1.clone.clone.clone.1 | convolution fusion | flops 68736253952 | bytes 75497472 | tf_op jit(solution)/shard_map/dot_general | solution.py:15
  311.7 0.0 all-gather.5.cloned.1.call-done
  311.7 24.7 %fusion.15 = f32[64,4,64]{0,2,1:T(8,128)} fusion(bf16[64,128,512]{2,0,1:T(8,128)(2,1)} %all-gather.5.cloned.1.call-done, bf16[64,128,4,512]{3,0,1,2:T(8,128)(2,1)} %fusion.33), kind=kOutput, calls=%fused_computation.8 | convolution fusion | flops 2147483648 | bytes 42008576 | tf_op jit(solution)/shard_map/dot_general | solution.py:21
  336.5 0.0 reduce-scatter.2.cloned.1.call-update
  336.5 17.8 %reduce-scatter.2.cloned.1.call-done = f32[64,4,16]{0,2,1:T(8,128)} async-done(((f32[64,4,64]{0,2,1:T(8,128)}), f32[64,4,16]{0,2,1:T(8,128)}) %reduce-scatter.2.cloned.1.call-update) | async-done | bytes 16400 | tf_op jit(solution)/shard_map/reduce_scatter | solution.py:33
Async XLA Ops:
  6.5 68.6 %copy-start = (bf16[8,128,512]{2,1,0:T(8,128)(2,1)S(1)}, bf16[8,128,512]{2,1,0:T(8,128)(2,1)}, u32[]{:S(2)}) copy-start(bf16[8,128,512]{2,1,0:T(8,128)(2,1)} %param.2) | copy-start | bytes 3145732
  6.5 68.5 %all-reduce.2.cloned.1.call-start = ((), (), s32[]{:S(2)}) async-start(), calls=%async_computation.1 | async-start | bytes 4194304 | tf_op jit(solution)/shard_map/psum | solution.py:11
  9.7 215.7 %all-gather.3.cloned.1.call-start = ((), (), s32[]{:S(2)}) async-start(), calls=%async_computation.2 | async-start | bytes 10485760 | tf_op jit(solution)/shard_map/all_gather | solution.py:31
  75.1 236.6 %all-gather.5.cloned.1.call-start = ((), (), s32[]{:S(2)}) async-start(), calls=%async_computation.3 | async-start | bytes 9437184 | tf_op jit(solution)/shard_map/all_gather | solution.py:28
  76.7 277.5 %reduce-scatter.2.cloned.1.call-start = ((), (), s32[]{:S(2)}) async-start(), calls=%async_computation.4 | async-start | bytes 163840 | tf_op jit(solution)/shard_map/reduce_scatter | solution.py:33
Sparse Core Ops, SparseCore 0:
  10.6 64.4 all-reduce.1
  76.6 148.6 all-gather.2
  227.3 54.0 all-gather.4
  336.6 17.6 reduce-scatter.1
where the time goes:
time: 361 us
  waiting for transfers between devices  232 us (64%)
  matrix products  111 us (31%)
  between operations  13.1 us (4%)
    all_gather x1, waiting for transfers between devices, per_device(): lax.all_gather(shared, 'grp', axis=1, tiled=True)  149 us
    dot_general x1, matrix products, build_tile(): lax.dot_general(chol_local, portion, (((2,), (2,)), ((), ())), preferred_...  86.3 us
    psum x1, waiting for transfers between devices, spread(): return lax.psum(kept, axis)  65.3 us
    dot_general x1, matrix products, ladder(): lax.dot_general(integrals, amp_part, (((1, 3), (1, 2)), ((), ())), prefer...  24.7 us
    reduce_scatter x1, waiting for transfers between devices, per_device(): return lax.psum_scatter(summed, 'grp', scatter_dimension=2, tiled=True)  17.8 us
  transfers between devices with their start and end apart: 4, of which 3 were waited for; matrix products, arithmetic and copies ran while one was open for 24% of the time, Pallas kernels for 0%

commit v1 on v0

--- a/solution.py
+++ b/solution.py
@@ -8,7 +8,7 @@
 
 def spread(value, axis, source):
     kept = jnp.where(lax.axis_index(axis) == source, value, 0).astype(value.dtype)
-    return lax.psum(kept, axis)
+    return jnp.sum(lax.all_gather(kept, axis), axis=0)
 
 
 def build_tile(chol_local, portion):

time: 361 us -> 399 us (1.11)
  waiting for transfers between devices: 232 us -> 258 us
  other arithmetic: 3.13 us -> 14 us
    all_gather x0 -> x1, waiting for transfers between devices: none -> 92.6 us  [spread(): return jnp.sum(lax.all_gather(kept, axis), axis=0)]
    psum x1 -> x0, waiting for transfers between devices: 65.3 us -> none  [spread(): return lax.psum(kept, axis)]
    reduce_sum x0 -> x1, other arithmetic: none -> 10.8 us  [spread(): return jnp.sum(lax.all_gather(kept, axis), axis=0)]
  transfers between devices with their start and end apart: 4 -> 4, of which waited for: 3 -> 3; matrix products, arithmetic and copies ran while one was open for 24% -> 22% of each run, Pallas kernels for 0% -> 0%
where the time goes in v1:
time: 399 us; the launch traced here: 398 us
  waiting for transfers between devices  258 us (65%)
  matrix products  111 us (28%)
  other arithmetic  14 us (4%)
  between operations  13.1 us (3%)
    all_gather x1, waiting for transfers between devices, per_device(): lax.all_gather(shared, 'grp', axis=1, tiled=True)  148 us
    all_gather x1, waiting for transfers between devices, spread(): return jnp.sum(lax.all_gather(kept, axis), axis=0)  92.6 us
    dot_general x1, matrix products, build_tile(): lax.dot_general(chol_local, portion, (((2,), (2,)), ((), ())), preferred_...  86.3 us
    dot_general x1, matrix products, ladder(): lax.dot_general(integrals, amp_part, (((1, 3), (1, 2)), ((), ())), prefer...  24.7 us
    reduce_scatter x1, waiting for transfers between devices, per_device(): return lax.psum_scatter(summed, 'grp', scatter_dimension=2, tiled=True)  17.8 us
    reduce_sum x1, other arithmetic, spread(): return jnp.sum(lax.all_gather(kept, axis), axis=0)  10.8 us
  transfers between devices with their start and end apart: 4, of which 3 were waited for; matrix products, arithmetic and copies ran while one was open for 22% of the time, Pallas kernels for 0%

profile of v1, /device:TPU:0, one launch (start us, length us, event | category | flops | bytes accessed | tf_op | source)
XLA Modules:
  0.0 398.4 jit_solution(10439906688226896538)
XLA Ops:
  6.5 0.0 copy-start
  6.5 0.0 all-gather.9.cloned.1.call-start
  6.5 3.2 slice_select_fusion
  9.7 0.0 all-gather.9.cloned.1.call-update
  9.7 0.0 all-gather.5.cloned.1.call-start
  9.8 92.6 %all-gather.9.cloned.1.call-done = bf16[32,128,2048]{2,1,0:T(8,128)(2,1)} async-done(((bf16[4,128,2048]{2,1,0:T(8,128)(2,1)}), bf16[32,128,2048]{2,1,0:T(8,128)(2,1)}) %all-gather.9.cloned.1.call-update) | async-done | bytes 16777232 | tf_op jit(solution)/shard_map/all_gather | solution.py:11
  102.3 10.8 %reduce_sum.12 = bf16[4,128,2048]{2,1,0:T(8,128)(2,1)} reduce(bf16[8,4,128,2048]{3,2,1,0:T(8,128)(2,1)} %bitcast.35, bf16[]{:T(256)} %constant.9.clone.1), dimensions={0}, to_apply=%region_0.1 | reduce | flops 7340032 | bytes 18874370 | tf_op jit(solution)/shard_map/reduce_sum | solution.py:11
  113.2 0.0 all-gather.5.cloned.1.call-update
  113.2 0.0 all-gather.7.cloned.1.call-start
  113.2 0.0 copy-done
  113.2 1.6 copy.4
  114.8 0.0 all-gather.7.cloned.1.call-update
  114.8 0.0 reduce-scatter.2.cloned.1.call-start
  114.9 148.1 %all-gather.5.cloned.1.call-done = bf16[4,512,2048]{2,1,0:T(8,128)(2,1)} async-done(((bf16[4,128,2048]{2,1,0:T(8,128)(2,1)}), bf16[4,512,2048]{2,1,0:T(8,128)(2,1)}) %all-gather.5.cloned.1.call-update) | async-done | bytes 8388624 | tf_op jit(solution)/shard_map/all_gather | solution.py:31
  262.9 86.3 %fusion.33 = bf16[64,128,4,512]{3,0,1,2:T(8,128)(2,1)} fusion(bf16[64,128,2048,1]{2,1,0,3:T(8,128)(2,1)} %bitcast.36, bf16[4,512,2048]{2,1,0:T(8,128)(2,1)} %all-gather.5.cloned.1.call-done), kind=kOutput, calls=%fused_computation.1.clone.clone.clone.1 | convolution fusion | flops 68736253952 | bytes 75497472 | tf_op jit(solution)/shard_map/dot_general | solution.py:15
  349.3 0.0 all-gather.7.cloned.1.call-done
  349.3 24.7 %fusion.15 = f32[64,4,64]{0,2,1:T(8,128)} fusion(bf16[64,128,512]{2,0,1:T(8,128)(2,1)} %all-gather.7.cloned.1.call-done, bf16[64,128,4,512]{3,0,1,2:T(8,128)(2,1)} %fusion.33), kind=kOutput, calls=%fused_computation.8 | convolution fusion | flops 2147483648 | bytes 42008576 | tf_op jit(solution)/shard_map/dot_general | solution.py:21
  374.0 0.0 reduce-scatter.2.cloned.1.call-update
  374.1 17.8 %reduce-scatter.2.cloned.1.call-done = f32[64,4,16]{0,2,1:T(8,128)} async-done(((f32[64,4,64]{0,2,1:T(8,128)}), f32[64,4,16]{0,2,1:T(8,128)}) %reduce-scatter.2.cloned.1.call-update) | async-done | bytes 16400 | tf_op jit(solution)/shard_map/reduce_scatter | solution.py:33
Async XLA Ops:
  6.5 106.7 %copy-start = (bf16[8,128,512]{2,1,0:T(8,128)(2,1)S(1)}, bf16[8,128,512]{2,1,0:T(8,128)(2,1)}, u32[]{:S(2)}) copy-start(bf16[8,128,512]{2,1,0:T(8,128)(2,1)} %param.2) | copy-start | bytes 3145732
  6.5 95.8 %all-gather.9.cloned.1.call-start = ((), (), s32[]{:S(2)}) async-start(), calls=%async_computation.4 | async-start | bytes 18874368 | tf_op jit(solution)/shard_map/all_gather | solution.py:11
  9.7 253.2 %all-gather.5.cloned.1.call-start = ((), (), s32[]{:S(2)}) async-start(), calls=%async_computation.1 | async-start | bytes 10485760 | tf_op jit(solution)/shard_map/all_gather | solution.py:31
  113.2 236.1 %all-gather.7.cloned.1.call-start = ((), (), s32[]{:S(2)}) async-start(), calls=%async_computation.2 | async-start | bytes 9437184 | tf_op jit(solution)/shard_map/all_gather | solution.py:28
  114.8 277.0 %reduce-scatter.2.cloned.1.call-start = ((), (), s32[]{:S(2)}) async-start(), calls=%async_computation.3 | async-start | bytes 163840 | tf_op jit(solution)/shard_map/reduce_scatter | solution.py:33
Sparse Core Ops, SparseCore 0:
  9.8 92.4 all-gather.8
  113.3 149.5 all-gather.4
  264.8 54.0 all-gather.6
  374.2 17.6 reduce-scatter.1
